TPU v7x, 32 devices: a whole 2x2x4 slice. The times are simulated.
32 devices in a mesh: tm: 8 (over z, y), series: 4 (over x, core).
Axes of the slice: x: 2, y: 2, z: 4, core: 2. Of those that a mesh axis runs over, the one named last changes fastest.
Arguments:
- signal: float32 [64, 262144], P('series', 'tm')
- valid_start: int32 [64], replicated, may hold values from 0 to 65535
- valid_end: int32 [64], replicated, may hold values from 196609 to 262144
Outputs:
- smooth: float32 [64, 262144], P('series', 'tm')
- slope: float32 [64, 262144], P('series', 'tm')
- covariance: float32 [64, 64], P('series')
Inputs may be any that keep to these rules, and one draw needn't show every extreme that they name: `valid_end`: end of the valid samples of each series.
All inputs are finite; a program needn't handle non-finite values.
Results may differ from a plain program's by a relative error of at most 0.00015.
Values sent between devices are 32-bit elements; how exact they have to be, the bound alone decides.
A program may use at most 64 MiB of HBM per device.

v0:
```python
import functools

import jax
import jax.numpy as jnp
from jax import lax
from jax.experimental import pallas as pl
from jax.experimental.pallas import tpu as pltpu
from jax.sharding import PartitionSpec as P

HALF = 16
LANE = 128
TAPS = 2 * HALF + 1
SECOND = float(sum(j * j for j in range(-HALF, HALF + 1)))
CENTRE_SQ = SECOND / TAPS
FOURTH = float(sum((j * j - CENTRE_SQ) ** 2 for j in range(-HALF, HALF + 1)))
MESH = pl.DeviceIdType.MESH


def chunk_of(quarter):
    chunk = 1024
    while quarter % chunk:
        chunk //= 2
    return chunk


def kernel(
    n_s, n_t, rows, width, chunk,
    bounds_hbm, sig_hbm,
    smooth, slope, cov,
    bounds, ext, wts, ends, res, mixed, halo, part, r1, mine, r2,
    load_sem, bound_sem, halo_send, halo_recv, send_sem, recv_sem, s1_send, s1_recv, s2_send, s2_recv,
):
    s = lax.axis_index("series")
    t = lax.axis_index("tm")
    quarter = width // n_s
    per = quarter // chunk
    steps = n_s * per
    sends = (n_s - 1) * per
    total = n_s * rows
    tiles = chunk // LANE
    f32 = jnp.float32

    limits = pltpu.make_async_copy(bounds_hbm, bounds, bound_sem)
    limits.start()
    def offset(qi):
        if n_s == 4:
            odd = lax.rem(s, 2)
            return jnp.where(qi == 0, 2, jnp.where(qi == 1, 3 - 2 * odd, jnp.where(qi == 2, 1 + 2 * odd, 0)))
        return lax.rem(qi + 1, n_s)

    def load(qi):
        q = lax.rem(s + offset(qi), n_s)
        return pltpu.make_async_copy(
            sig_hbm.at[:, pl.ds(pl.multiple_of(q * quarter, LANE), quarter)],
            ext.at[:, pl.ds(pl.multiple_of(q * quarter + LANE, LANE), quarter)],
            load_sem.at[qi])

    for qi in range(n_s):
        load(qi).start()
    barrier = pltpu.get_barrier_semaphore()
    for d in range(1, n_s):
        pl.semaphore_signal(barrier, inc=1, device_id={"series": lax.rem(s + d, n_s)}, device_id_type=MESH)
    for d in range(1, n_t):
        pl.semaphore_signal(barrier, inc=1, device_id={"tm": lax.rem(t + d, n_t)}, device_id_type=MESH)

    tap = lax.broadcasted_iota(jnp.int32, (2 * LANE, LANE), 0) - lax.broadcasted_iota(jnp.int32, (2 * LANE, LANE), 1) - HALF
    near = (tap >= -HALF) & (tap <= HALF)
    tap = tap.astype(f32)
    wts[:, :LANE] = jnp.where(near, 1.0 / TAPS - (tap * tap - CENTRE_SQ) * (CENTRE_SQ / FOURTH), 0.0)
    wts[:, LANE:] = jnp.where(near, tap * (HALF / SECOND), 0.0)
    ext[:, :LANE] = jnp.zeros((rows, LANE), f32)
    ext[:, LANE + width :] = jnp.zeros((rows, LANE), f32)

    limits.wait()
    row = lax.broadcasted_iota(jnp.int32, (rows, LANE), 0)
    begin = t * width
    first = jnp.zeros((rows, LANE), jnp.int32)
    last = jnp.zeros((rows, LANE), jnp.int32)
    for i in range(rows):
        first = jnp.where(row == i, bounds[0, s * rows + i], first)
        last = jnp.where(row == i, bounds[1, s * rows + i], last)
    ends[0] = first - begin
    ends[1] = last - begin

    def held(v, base):
        lanes = lax.broadcasted_iota(jnp.int32, (rows, LANE), 1)
        found = []
        for spot in (ends[0] + LANE - base, ends[1] - TAPS + LANE - base):
            tile = lax.shift_right_arithmetic(spot, LANE.bit_length() - 1)
            pair = [jnp.zeros((rows, LANE), f32)] * 2
            for n in range(tiles + 1):
                here = tile == n
                for w in range(2):
                    pair[w] = jnp.where(here, v[:, (n + w) * LANE : (n + w + 1) * LANE], pair[w])
            j = lanes - (spot - tile * LANE + HALF)
            sums = []
            for j, win in ((j, pair[0]), (j + LANE, pair[1])):
                win = jnp.where((j >= -HALF) & (j <= HALF), win, 0.0)
                j = j.astype(f32)
                sums.append((win, win * j, win * (j * j - CENTRE_SQ)))
            for m, scale in enumerate((1.0 / TAPS, 1.0 / SECOND, 1.0 / FOURTH)):
                value = jnp.sum(sums[0][m] + sums[1][m], axis=1, keepdims=True) * scale
                found.append(jnp.broadcast_to(value, (rows, LANE)))
        return found

    right, left = lax.rem(t + 1, n_t), lax.rem(t + n_t - 1, n_t)
    to_right = pltpu.make_async_remote_copy(
        ext.at[:, pl.ds(width, LANE)], halo.at[0], halo_send.at[0], halo_recv.at[0],
        device_id={"tm": right}, device_id_type=MESH)
    to_left = pltpu.make_async_remote_copy(
        ext.at[:, pl.ds(LANE, LANE)], halo.at[1], halo_send.at[1], halo_recv.at[1],
        device_id={"tm": left}, device_id_type=MESH)
    def place(k):
        qi = k // per
        q = lax.rem(s + offset(qi), n_s)
        j = lax.rem(lax.rem(k, per) + 1, per)
        return q, j

    def transfer(k):
        q, j = place(k)
        return pltpu.make_async_remote_copy(
            res.at[:, pl.ds(pl.multiple_of(q * quarter + j * chunk, chunk), chunk)],
            mixed.at[s, :, pl.ds(pl.multiple_of(j * chunk, chunk), chunk)],
            send_sem.at[k], recv_sem.at[k],
            device_id={"series": q}, device_id_type=MESH)

    def spread(v):
        return jnp.concatenate([v] * tiles, axis=1)

    def step(k, carry):
        @pl.when(k == 0)
        def _():
            load(0).wait()

        @pl.when(k == 1)
        def _():
            for qi in range(1, n_s):
                load(qi).wait()

        @pl.when(k == per - 2)
        def _():
            to_right.wait_recv()
            to_left.wait_recv()
            ext[:, :LANE] = jnp.where(t == 0, 0.0, halo[0])
            ext[:, LANE + width :] = jnp.where(t == n_t - 1, 0.0, halo[1])

        q, j = place(k)
        base = pl.multiple_of(q * quarter + j * chunk, chunk)
        v = ext[:, pl.ds(base, chunk + 2 * LANE)]
        moved = pltpu.roll(v, chunk + LANE + HALF, 1)
        lines = jnp.concatenate([moved[:, n * LANE : (n + 2) * LANE] for n in range(tiles)], axis=0)
        out = jnp.dot(lines, wts[...], precision=lax.Precision.HIGHEST, preferred_element_type=f32)
        sm = jnp.concatenate([out[n * rows : (n + 1) * rows, :LANE] for n in range(tiles)], axis=1)
        sl = jnp.concatenate([out[n * rows : (n + 1) * rows, LANE:] for n in range(tiles)], axis=1)
        moment = base + lax.broadcasted_iota(jnp.int32, (rows, chunk), 1)
        low = moment - spread(ends[0])
        high = moment - spread(ends[1])
        coef = held(v, base)
        inside = (low >= 0) & (high < 0)
        below = low < HALF
        above = high >= -HALF
        along = jnp.where(below, low - HALF, high + HALF + 1).astype(f32)
        lv = jnp.where(below, spread(coef[0]), spread(coef[3]))
        tl = jnp.where(below, spread(coef[1]), spread(coef[4]))
        bd = jnp.where(below, spread(coef[2]), spread(coef[5]))
        end = below | above
        sm = jnp.where(end, lv + tl * along + bd * (along * along - CENTRE_SQ), sm)
        sl = jnp.where(end, HALF * (tl + 2.0 * along * bd), sl)
        sm = jnp.where(inside, sm, 0.0)
        smooth[:, pl.ds(base, chunk)] = sm
        slope[:, pl.ds(base, chunk)] = jnp.where(inside, sl, 0.0)
        rs = jnp.where(inside, v[:, LANE : LANE + chunk] - sm, 0.0)

        @pl.when(k < sends)
        def _():
            res[:, pl.ds(base, chunk)] = rs

        @pl.when(k >= sends)
        def _():
            mixed[s, :, pl.ds(pl.multiple_of(j * chunk, chunk), chunk)] = rs

        @pl.when(k == 0)
        def _():
            pl.semaphore_wait(barrier, n_s - 1 + n_t - 1)

        @pl.when(k == 1)
        def _():
            to_right.start()
            to_left.start()

        @pl.when((k >= 1) & (k <= sends))
        def _():
            transfer(k - 1).start()

        return carry

    lax.fori_loop(0, steps, step, 0)

    def arrival(k, i):
        src = lax.rem(s + n_s - offset(k // per), n_s)
        j = (i + 1) % per
        return pltpu.make_async_remote_copy(
            res.at[:, pl.ds(0, chunk)],
            mixed.at[src, :, pl.ds(pl.multiple_of(j * chunk, chunk), chunk)],
            send_sem.at[k], recv_sem.at[k],
            device_id={"series": src}, device_id_type=MESH)

    half = rows // 2
    left_half = lax.broadcasted_iota(jnp.int32, (half, 2 * total), 1) < total

    def pack(v):
        return jnp.where(left_half, v[:half], v[half:])

    gram = jnp.zeros((2 * total, 2 * total), f32)
    for i in range(per):
        for qi in range(n_s - 1):
            arrival(qi * per + i, i).wait_recv()
        j = (i + 1) % per
        x = jnp.concatenate(
            [mixed[g, :, pl.ds(pl.multiple_of(j * chunk, chunk), chunk)] for g in range(n_s)], axis=0)
        hi = x.astype(jnp.bfloat16)
        lo = (x - hi.astype(f32)).astype(jnp.bfloat16)
        z = jnp.concatenate([hi, lo], axis=0)
        gram = gram + lax.dot_general(z, z, (((1,), (1,)), ((), ())), preferred_element_type=f32)
    both = gram[:total] + gram[total:]
    both = both + pltpu.roll(both, total, 1)
    for g in range(n_s):
        part[g] = pack(both[g * rows : (g + 1) * rows])

    def first_stage(d):
        peer = lax.rem(s + d, n_s)
        return pltpu.make_async_remote_copy(
            part.at[peer], r1.at[d - 1], s1_send.at[d - 1], s1_recv.at[d - 1],
            device_id={"series": peer}, device_id_type=MESH)

    for d in range(1, n_s):
        first_stage(d).start()

    lane = lax.broadcasted_iota(jnp.int32, (rows, 2 * total), 1)
    lane = jnp.where(lane < total, lane, lane - total)
    first_k = jnp.zeros((rows, 2 * total), jnp.int32)
    last_k = jnp.zeros((rows, 2 * total), jnp.int32)
    for i in range(total):
        first_k = jnp.where(lane == i, bounds[0, i], first_k)
        last_k = jnp.where(lane == i, bounds[1, i], last_k)
    count = pack((jnp.minimum(last_k, last) - jnp.maximum(first_k, first)).astype(f32))

    own = part[s]
    for d in range(1, n_s):
        first_stage(d).wait_recv()
        own = own + r1[d - 1]
    mine[...] = own

    def second_stage(d):
        return pltpu.make_async_remote_copy(
            mine, r2.at[t], s2_send.at[d - 1], s2_recv.at[d - 1],
            device_id={"tm": lax.rem(t + d, n_t)}, device_id_type=MESH)

    def second_arrival(d):
        src = lax.rem(t + n_t - d, n_t)
        return pltpu.make_async_remote_copy(
            mine, r2.at[src], s2_send.at[d - 1], s2_recv.at[d - 1],
            device_id={"tm": src}, device_id_type=MESH)

    for d in range(1, n_t):
        second_stage(d).start()
    r2[t] = own
    for k in range(sends):
        transfer(k).wait_send()
    to_right.wait_send()
    to_left.wait_send()
    for d in range(1, n_s):
        first_stage(d).wait_send()
    for d in range(1, n_t):
        second_arrival(d).wait_recv()
    full = r2[0]
    for d in range(1, n_t):
        full = full + r2[d]
    full = full / count
    cov[:half] = full[:, :total]
    cov[half:] = pltpu.roll(full, total, 1)[:, :total]
    for d in range(1, n_t):
        second_stage(d).wait_send()


FLUSHES = 4


def flush(smooth, slope, cov, smooth_out, slope_out, cov_out, sems, cov_sem):
    piece = smooth.shape[1] // FLUSHES
    copies = [pltpu.make_async_copy(cov, cov_out, cov_sem)]
    for i in range(FLUSHES):
        span = pl.ds(i * piece, piece)
        copies.append(pltpu.make_async_copy(smooth.at[:, span], smooth_out.at[:, span], sems.at[2 * i]))
        copies.append(pltpu.make_async_copy(slope.at[:, span], slope_out.at[:, span], sems.at[2 * i + 1]))
    for copy in copies:
        copy.start()
    for copy in copies:
        copy.wait()


def solution(mesh):
    n_t, n_s = mesh.shape["tm"], mesh.shape["series"]

    def shards(signal, valid_start, valid_end):
        rows, width = signal.shape
        total = rows * n_s
        quarter = width // n_s
        chunk = chunk_of(quarter)
        sends = (n_s - 1) * (quarter // chunk)
        f32 = jnp.float32
        dma = pltpu.SemaphoreType.DMA
        kept = pl.pallas_call(
            functools.partial(kernel, n_s, n_t, rows, width, chunk),
            out_shape=(
                jax.ShapeDtypeStruct((rows, width), f32),
                jax.ShapeDtypeStruct((rows, width), f32),
                jax.ShapeDtypeStruct((rows, total), f32),
            ),
            in_specs=[
                pl.BlockSpec(memory_space=pltpu.HBM),
                pl.BlockSpec(memory_space=pltpu.HBM),
            ],
            out_specs=(pl.BlockSpec(memory_space=pltpu.VMEM),) * 3,
            scratch_shapes=[
                pltpu.SMEM((2, total), jnp.int32),
                pltpu.VMEM((rows, width + 2 * LANE), f32),
                pltpu.VMEM((2 * LANE, 2 * LANE), f32),
                pltpu.VMEM((2, rows, LANE), jnp.int32),
                pltpu.VMEM((rows, width), f32),
                pltpu.VMEM((n_s, rows, quarter), f32),
                pltpu.VMEM((2, rows, LANE), f32),
                pltpu.VMEM((n_s, rows // 2, 2 * total), f32),
                pltpu.VMEM((n_s - 1, rows // 2, 2 * total), f32),
                pltpu.VMEM((rows // 2, 2 * total), f32),
                pltpu.VMEM((n_t, rows // 2, 2 * total), f32),
                dma((n_s,)),
                dma,
                dma((2,)),
                dma((2,)),
                dma((sends,)),
                dma((sends,)),
                dma((n_s - 1,)),
                dma((n_s - 1,)),
                dma((n_t - 1,)),
                dma((n_t - 1,)),
            ],
            compiler_params=pltpu.CompilerParams(
                collective_id=0, has_side_effects=True, vmem_limit_bytes=67043328 - 8 * rows * width - 12 * 1024 * 1024
            ),
        )(jnp.stack([valid_start, valid_end]), signal)
        return pl.pallas_call(
            flush,
            out_shape=tuple(jax.ShapeDtypeStruct(v.shape, f32) for v in kept),
            in_specs=[pl.BlockSpec(memory_space=pltpu.VMEM)] * 3,
            out_specs=(pl.BlockSpec(memory_space=pltpu.HBM),) * 3,
            scratch_shapes=[dma((2 * FLUSHES,)), dma],
            compiler_params=pltpu.CompilerParams(vmem_limit_bytes=1024 * 1024),
        )(*kept)

    in_specs = (P("series", "tm"), P(), P())
    out_specs = (P("series", "tm"), P("series", "tm"), P("series", None))
    return jax.shard_map(shards, mesh=mesh, in_specs=in_specs, out_specs=out_specs, check_vma=False)
```

profile of v0, /device:TPU:0, one launch (start us, length us, event | category | flops | bytes accessed | tf_op | source)
XLA Modules:
  0.0 40.5 jit_solution(8101620439161128931)
XLA Ops:
  0.6 0.7 %pad_add_fusion.bounds_hbm = s32[2,64]{1,0:T(2,128)S(1)} fusion(s32[1,64]{1,0:T(1,128)} %bitcast.2, s32[1,64]{1,0:T(1,128)} %bitcast.3), kind=kLoop, calls=%fused_computation | loop fusion | flops 128 | bytes 1024 | tf_op jit(solution)/shard_map/stack | solution.py:351
  1.3 37.1 %shard_map.58 = (f32[16,32768]{1,0:T(8,128)S(1)}, f32[16,32768]{1,0:T(8,128)S(1)}, f32[16,64]{1,0:T(8,128)S(1)}) custom-call(s32[2,64]{1,0:T(2,128)S(1)} %pad_add_fusion.bounds_hbm, f32[16,32768]{1,0:T(8,128)} %sig_hbm.1), custom_call_target="tpu_custom_call" | custom-call | tf_op jit(solution)/shard_map/pallas_call | solution.py:313
  38.5 2.1 %shard_map.59 = (f32[16,32768]{1,0:T(8,128)}, f32[16,32768]{1,0:T(8,128)}, f32[16,64]{1,0:T(8,128)}) custom-call(f32[16,32768]{1,0:T(8,128)S(1)} %get-tuple-element.6.smooth, f32[16,32768]{1,0:T(8,128)S(1)} %get-tuple-element.7.slope, f32[16,64]{1,0:T(8,128)S(1)} %get-tuple-element.8.cov), custom_call_target="tpu_custom_call" | custom-call | tf_op jit(solution)/shard_map/pallas_call | solution.py:352
where the time goes:
time: 40.7 us; the launch traced here: 40.5 us
  Pallas kernels  39.2 us (96%)
  other arithmetic  0.68 us (2%)
  between operations  0.64 us (2%)
    pallas_call x1, Pallas kernels, shards(): pl.pallas_call(functools.partial(kernel, n_s, n_t, rows, width, chunk), o...  37.1 us
    pallas_call x1, Pallas kernels, shards(): pl.pallas_call(flush, out_shape=tuple((jax.ShapeDtypeStruct(v.shape, f32)...  2.09 us

commit v1 on v0

--- a/solution.py
+++ b/solution.py
@@ -25,10 +25,10 @@
 
 def kernel(
     n_s, n_t, rows, width, chunk,
-    bounds_hbm, sig_hbm,
+    start_hbm, end_hbm, sig_hbm,
     smooth, slope, cov,
-    bounds, ext, wts, ends, res, mixed, halo, part, r1, mine, r2,
-    load_sem, bound_sem, halo_send, halo_recv, send_sem, recv_sem, s1_send, s1_recv, s2_send, s2_recv,
+    starts, stops, ext, wts, ends, res, mixed, halo, part, r1, mine, r2,
+    load_sem, bound_sem, halo_send, halo_recv, send_sem, recv_sem, s1_sem, s2_sem, met,
 ):
     s = lax.axis_index("series")
     t = lax.axis_index("tm")
@@ -38,30 +38,62 @@
     sends = (n_s - 1) * per
     total = n_s * rows
     tiles = chunk // LANE
+    group = 2 - n_t % 2
     f32 = jnp.float32
 
-    limits = pltpu.make_async_copy(bounds_hbm, bounds, bound_sem)
-    limits.start()
     def offset(qi):
         if n_s == 4:
             odd = lax.rem(s, 2)
             return jnp.where(qi == 0, 2, jnp.where(qi == 1, 3 - 2 * odd, jnp.where(qi == 2, 1 + 2 * odd, 0)))
         return lax.rem(qi + 1, n_s)
 
-    def load(qi):
-        q = lax.rem(s + offset(qi), n_s)
+    def fetch(at, size, sem):
         return pltpu.make_async_copy(
-            sig_hbm.at[:, pl.ds(pl.multiple_of(q * quarter, LANE), quarter)],
-            ext.at[:, pl.ds(pl.multiple_of(q * quarter + LANE, LANE), quarter)],
-            load_sem.at[qi])
-
-    for qi in range(n_s):
-        load(qi).start()
+            sig_hbm.at[:, pl.ds(pl.multiple_of(at, LANE), size)],
+            ext.at[:, pl.ds(pl.multiple_of(at + LANE, LANE), size)],
+            load_sem.at[sem])
+
+    head = lax.rem(s + offset(0), n_s) * quarter
+    lead = min(chunk + 2 * LANE, quarter - chunk + LANE)
+    before = chunk - LANE
+    after = quarter - before - lead
+    fetch(head + before, lead, 0).start()
+
+    partner = t + 1 - 2 * lax.rem(t, 2)
+
+    def tell(sem, at, ok=None):
+        def signal():
+            pl.semaphore_signal(sem, inc=1, device_id={"tm": at}, device_id_type=MESH)
+        if ok is None:
+            signal()
+        else:
+            pl.when(ok)(signal)
+
+    def reach(sem, far):
+        tell(sem, t - far, t >= far)
+        tell(sem, t + far, t + far < n_t)
+
+    def heard(far):
+        return (t >= far).astype(jnp.int32) + (t + far < n_t).astype(jnp.int32)
+
     barrier = pltpu.get_barrier_semaphore()
     for d in range(1, n_s):
         pl.semaphore_signal(barrier, inc=1, device_id={"series": lax.rem(s + d, n_s)}, device_id_type=MESH)
-    for d in range(1, n_t):
-        pl.semaphore_signal(barrier, inc=1, device_id={"tm": lax.rem(t + d, n_t)}, device_id_type=MESH)
+    if group == 2:
+        tell(barrier, partner)
+    reach(barrier, group)
+
+    limits = [
+        pltpu.make_async_copy(start_hbm, starts, bound_sem.at[0]),
+        pltpu.make_async_copy(end_hbm, stops, bound_sem.at[1]),
+    ]
+    for limit in limits:
+        limit.start()
+    fetch(head, before, 1).start()
+    if after:
+        fetch(head + before + lead, after, 1).start()
+    for qi in range(1, n_s):
+        fetch(lax.rem(s + offset(qi), n_s) * quarter, quarter, 1).start()
 
     tap = lax.broadcasted_iota(jnp.int32, (2 * LANE, LANE), 0) - lax.broadcasted_iota(jnp.int32, (2 * LANE, LANE), 1) - HALF
     near = (tap >= -HALF) & (tap <= HALF)
@@ -71,14 +103,15 @@
     ext[:, :LANE] = jnp.zeros((rows, LANE), f32)
     ext[:, LANE + width :] = jnp.zeros((rows, LANE), f32)
 
-    limits.wait()
+    for limit in limits:
+        limit.wait()
     row = lax.broadcasted_iota(jnp.int32, (rows, LANE), 0)
     begin = t * width
     first = jnp.zeros((rows, LANE), jnp.int32)
     last = jnp.zeros((rows, LANE), jnp.int32)
     for i in range(rows):
-        first = jnp.where(row == i, bounds[0, s * rows + i], first)
-        last = jnp.where(row == i, bounds[1, s * rows + i], last)
+        first = jnp.where(row == i, starts[s * rows + i], first)
+        last = jnp.where(row == i, stops[s * rows + i], last)
     ends[0] = first - begin
     ends[1] = last - begin
 
@@ -110,6 +143,8 @@
     to_left = pltpu.make_async_remote_copy(
         ext.at[:, pl.ds(LANE, LANE)], halo.at[1], halo_send.at[1], halo_recv.at[1],
         device_id={"tm": left}, device_id_type=MESH)
+    has_right, has_left = t < n_t - 1, t > 0
+
     def place(k):
         qi = k // per
         q = lax.rem(s + offset(qi), n_s)
@@ -121,28 +156,34 @@
         return pltpu.make_async_remote_copy(
             res.at[:, pl.ds(pl.multiple_of(q * quarter + j * chunk, chunk), chunk)],
             mixed.at[s, :, pl.ds(pl.multiple_of(j * chunk, chunk), chunk)],
-            send_sem.at[k], recv_sem.at[k],
+            send_sem, recv_sem.at[j],
             device_id={"series": q}, device_id_type=MESH)
 
     def spread(v):
         return jnp.concatenate([v] * tiles, axis=1)
 
+    greet = min(3, per - 3)
+
     def step(k, carry):
         @pl.when(k == 0)
         def _():
-            load(0).wait()
+            fetch(0, lead, 0).wait()
 
         @pl.when(k == 1)
         def _():
-            for qi in range(1, n_s):
-                load(qi).wait()
+            fetch(0, width - lead, 1).wait()
 
         @pl.when(k == per - 2)
         def _():
-            to_right.wait_recv()
-            to_left.wait_recv()
-            ext[:, :LANE] = jnp.where(t == 0, 0.0, halo[0])
-            ext[:, LANE + width :] = jnp.where(t == n_t - 1, 0.0, halo[1])
+            @pl.when(has_left)
+            def _():
+                to_right.wait_recv()
+                ext[:, :LANE] = halo[0]
+
+            @pl.when(has_right)
+            def _():
+                to_left.wait_recv()
+                ext[:, LANE + width :] = halo[1]
 
         q, j = place(k)
         base = pl.multiple_of(q * quarter + j * chunk, chunk)
@@ -181,12 +222,22 @@
 
         @pl.when(k == 0)
         def _():
-            pl.semaphore_wait(barrier, n_s - 1 + n_t - 1)
-
-        @pl.when(k == 1)
-        def _():
-            to_right.start()
-            to_left.start()
+            pl.semaphore_wait(barrier, n_s - 1 + group - 1 + heard(group))
+            if group == 2:
+                tell(met.at[0], partner)
+            reach(met.at[0], group)
+
+        @pl.when(k == greet)
+        def _():
+            pl.semaphore_wait(met.at[0], group - 1 + heard(group))
+
+            @pl.when(has_right)
+            def _():
+                to_right.start()
+
+            @pl.when(has_left)
+            def _():
+                to_left.start()
 
         @pl.when((k >= 1) & (k <= sends))
         def _():
@@ -196,14 +247,35 @@
 
     lax.fori_loop(0, steps, step, 0)
 
-    def arrival(k, i):
-        src = lax.rem(s + n_s - offset(k // per), n_s)
+    rounds = []
+    far = 2 * group
+    while far < n_t:
+        rounds.append(far)
+        far *= 2
+    rounds.append(0)
+
+    def greeting(i):
+        if i > len(rounds):
+            return
+        if i > 0:
+            far = rounds[i - 1]
+            if far:
+                pl.semaphore_wait(met.at[i], heard(far))
+            elif group == 2:
+                pl.semaphore_wait(met.at[i], 1)
+        if i < len(rounds):
+            far = rounds[i]
+            if far:
+                reach(met.at[i + 1], far)
+            elif group == 2:
+                tell(met.at[i + 1], partner)
+
+    def arrival(i):
         j = (i + 1) % per
+        block = mixed.at[pl.ds(0, n_s - 1), :, pl.ds(pl.multiple_of(j * chunk, chunk), chunk)]
         return pltpu.make_async_remote_copy(
-            res.at[:, pl.ds(0, chunk)],
-            mixed.at[src, :, pl.ds(pl.multiple_of(j * chunk, chunk), chunk)],
-            send_sem.at[k], recv_sem.at[k],
-            device_id={"series": src}, device_id_type=MESH)
+            block, block, send_sem, recv_sem.at[j],
+            device_id={"series": lax.rem(s + 1, n_s)}, device_id_type=MESH)
 
     half = rows // 2
     left_half = lax.broadcasted_iota(jnp.int32, (half, 2 * total), 1) < total
@@ -213,8 +285,8 @@
 
     gram = jnp.zeros((2 * total, 2 * total), f32)
     for i in range(per):
-        for qi in range(n_s - 1):
-            arrival(qi * per + i, i).wait_recv()
+        greeting(i)
+        arrival(i).wait_recv()
         j = (i + 1) % per
         x = jnp.concatenate(
             [mixed[g, :, pl.ds(pl.multiple_of(j * chunk, chunk), chunk)] for g in range(n_s)], axis=0)
@@ -222,6 +294,8 @@
         lo = (x - hi.astype(f32)).astype(jnp.bfloat16)
         z = jnp.concatenate([hi, lo], axis=0)
         gram = gram + lax.dot_general(z, z, (((1,), (1,)), ((), ())), preferred_element_type=f32)
+    for i in range(per, len(rounds) + 1):
+        greeting(i)
     both = gram[:total] + gram[total:]
     both = both + pltpu.roll(both, total, 1)
     for g in range(n_s):
@@ -230,7 +304,7 @@
     def first_stage(d):
         peer = lax.rem(s + d, n_s)
         return pltpu.make_async_remote_copy(
-            part.at[peer], r1.at[d - 1], s1_send.at[d - 1], s1_recv.at[d - 1],
+            part.at[peer], r1.at[d - 1], s1_sem.at[0], s1_sem.at[1],
             device_id={"series": peer}, device_id_type=MESH)
 
     for d in range(1, n_s):
@@ -241,46 +315,50 @@
     first_k = jnp.zeros((rows, 2 * total), jnp.int32)
     last_k = jnp.zeros((rows, 2 * total), jnp.int32)
     for i in range(total):
-        first_k = jnp.where(lane == i, bounds[0, i], first_k)
-        last_k = jnp.where(lane == i, bounds[1, i], last_k)
+        first_k = jnp.where(lane == i, starts[i], first_k)
+        last_k = jnp.where(lane == i, stops[i], last_k)
     count = pack((jnp.minimum(last_k, last) - jnp.maximum(first_k, first)).astype(f32))
 
+    def gather(ref, sems):
+        return pltpu.make_async_remote_copy(
+            ref, ref, sems.at[0], sems.at[1], device_id={"series": lax.rem(s + 1, n_s)}, device_id_type=MESH)
+
     own = part[s]
+    gather(r1, s1_sem).wait_recv()
     for d in range(1, n_s):
-        first_stage(d).wait_recv()
         own = own + r1[d - 1]
     mine[...] = own
 
     def second_stage(d):
         return pltpu.make_async_remote_copy(
-            mine, r2.at[t], s2_send.at[d - 1], s2_recv.at[d - 1],
+            mine, r2.at[t], s2_sem.at[0], s2_sem.at[1],
             device_id={"tm": lax.rem(t + d, n_t)}, device_id_type=MESH)
-
-    def second_arrival(d):
-        src = lax.rem(t + n_t - d, n_t)
-        return pltpu.make_async_remote_copy(
-            mine, r2.at[src], s2_send.at[d - 1], s2_recv.at[d - 1],
-            device_id={"tm": src}, device_id_type=MESH)
 
     for d in range(1, n_t):
         second_stage(d).start()
     r2[t] = own
-    for k in range(sends):
-        transfer(k).wait_send()
-    to_right.wait_send()
-    to_left.wait_send()
-    for d in range(1, n_s):
-        first_stage(d).wait_send()
-    for d in range(1, n_t):
-        second_arrival(d).wait_recv()
+    sent = res.at[:, pl.ds(0, sends * chunk)]
+    pltpu.make_async_remote_copy(
+        sent, sent, send_sem, recv_sem.at[0],
+        device_id={"series": lax.rem(s + 1, n_s)}, device_id_type=MESH).wait_send()
+
+    @pl.when(has_right)
+    def _():
+        to_right.wait_send()
+
+    @pl.when(has_left)
+    def _():
+        to_left.wait_send()
+
+    gather(r1, s1_sem).wait_send()
+    gather(r2.at[pl.ds(0, n_t - 1)], s2_sem).wait_recv()
     full = r2[0]
     for d in range(1, n_t):
         full = full + r2[d]
     full = full / count
     cov[:half] = full[:, :total]
     cov[half:] = pltpu.roll(full, total, 1)[:, :total]
-    for d in range(1, n_t):
-        second_stage(d).wait_send()
+    gather(r2.at[pl.ds(0, n_t - 1)], s2_sem).wait_send()
 
 
 FLUSHES = 4
@@ -307,7 +385,7 @@
         total = rows * n_s
         quarter = width // n_s
         chunk = chunk_of(quarter)
-        sends = (n_s - 1) * (quarter // chunk)
+        per = quarter // chunk
         f32 = jnp.float32
         dma = pltpu.SemaphoreType.DMA
         kept = pl.pallas_call(
@@ -317,13 +395,11 @@
                 jax.ShapeDtypeStruct((rows, width), f32),
                 jax.ShapeDtypeStruct((rows, total), f32),
             ),
-            in_specs=[
-                pl.BlockSpec(memory_space=pltpu.HBM),
-                pl.BlockSpec(memory_space=pltpu.HBM),
-            ],
+            in_specs=[pl.BlockSpec(memory_space=pltpu.HBM)] * 3,
             out_specs=(pl.BlockSpec(memory_space=pltpu.VMEM),) * 3,
             scratch_shapes=[
-                pltpu.SMEM((2, total), jnp.int32),
+                pltpu.SMEM((total,), jnp.int32),
+                pltpu.SMEM((total,), jnp.int32),
                 pltpu.VMEM((rows, width + 2 * LANE), f32),
                 pltpu.VMEM((2 * LANE, 2 * LANE), f32),
                 pltpu.VMEM((2, rows, LANE), jnp.int32),
@@ -334,21 +410,20 @@
                 pltpu.VMEM((n_s - 1, rows // 2, 2 * total), f32),
                 pltpu.VMEM((rows // 2, 2 * total), f32),
                 pltpu.VMEM((n_t, rows // 2, 2 * total), f32),
-                dma((n_s,)),
+                dma((2,)),
+                dma((2,)),
+                dma((2,)),
+                dma((2,)),
                 dma,
-                dma((2,)),
-                dma((2,)),
-                dma((sends,)),
-                dma((sends,)),
-                dma((n_s - 1,)),
-                dma((n_s - 1,)),
-                dma((n_t - 1,)),
-                dma((n_t - 1,)),
+                dma((per,)),
+                dma((2,)),
+                dma((2,)),
+                pltpu.SemaphoreType.REGULAR((n_t.bit_length() + 1,)),
             ],
             compiler_params=pltpu.CompilerParams(
                 collective_id=0, has_side_effects=True, vmem_limit_bytes=67043328 - 8 * rows * width - 12 * 1024 * 1024
             ),
-        )(jnp.stack([valid_start, valid_end]), signal)
+        )(valid_start, valid_end, signal)
         return pl.pallas_call(
             flush,
             out_shape=tuple(jax.ShapeDtypeStruct(v.shape, f32) for v in kept),

time: 40.7 us -> 40.8 us (level)
  local copies, waits for them, and re-layouts: 0 us -> 1.3 us
  other arithmetic: 0.68 us -> 0 us
  Pallas kernels: 39.2 us -> 38.6 us
    unnamed x0 -> x4, local copies, waits for them, and re-layouts: none -> 1.3 us
    another operation x1 -> x0, other arithmetic: 0.68 us -> none  [shards(): jnp.stack([valid_start, valid_end])]
    pallas_call x1, Pallas kernels: 37.1 us -> 36.6 us  [shards(): pl.pallas_call(functools.partial(kernel, n_s, n_t, rows, width, chunk), o...]
where the time goes in v1:
time: 40.8 us; the launch traced here: 40.6 us
  Pallas kernels  38.6 us (95%)
  local copies, waits for them, and re-layouts  1.3 us (3%)
  between operations  0.65 us (2%)
    pallas_call x1, Pallas kernels, shards(): pl.pallas_call(functools.partial(kernel, n_s, n_t, rows, width, chunk), o...  36.6 us
    pallas_call x1, Pallas kernels, shards(): pl.pallas_call(flush, out_shape=tuple((jax.ShapeDtypeStruct(v.shape, f32)...  2.09 us
    unnamed x4, local copies, waits for them, and re-layouts  1.3 us

profile of v1, /device:TPU:0, one launch (start us, length us, event | category | flops | bytes accessed | tf_op | source)
XLA Modules:
  0.0 40.6 jit_solution(17613151766189971363)
XLA Ops:
  0.6 0.0 copy-start
  0.6 0.6 %copy-done = s32[64]{0:T(128)S(1)} copy-done((s32[64]{0:T(128)S(1)}, s32[64]{0:T(128)}, u32[]{:S(2)}) %copy-start) | copy-done | bytes 280
  1.3 0.0 copy-start.1
  1.3 0.7 %copy-done.1 = s32[64]{0:T(128)S(1)} copy-done((s32[64]{0:T(128)S(1)}, s32[64]{0:T(128)}, u32[]{:S(2)}) %copy-start.1) | copy-done | bytes 280
  1.9 36.6 %shard_map.58 = (f32[16,32768]{1,0:T(8,128)S(1)}, f32[16,32768]{1,0:T(8,128)S(1)}, f32[16,64]{1,0:T(8,128)S(1)}) custom-call(s32[64]{0:T(128)S(1)} %copy-done, s32[64]{0:T(128)S(1)} %copy-done.1, f32[16,32768]{1,0:T(8,128)} %sig_hbm.1), custom_call_target="tpu_custom_call" | custom-call | tf_op jit(solution)/shard_map/pallas_call | solution.py:391
  38.5 2.1 %shard_map.59 = (f32[16,32768]{1,0:T(8,128)}, f32[16,32768]{1,0:T(8,128)}, f32[16,64]{1,0:T(8,128)}) custom-call(f32[16,32768]{1,0:T(8,128)S(1)} %get-tuple-element.6.smooth, f32[16,32768]{1,0:T(8,128)S(1)} %get-tuple-element.7.slope, f32[16,64]{1,0:T(8,128)S(1)} %get-tuple-element.8.cov), custom_call_target="tpu_custom_call" | custom-call | tf_op jit(solution)/shard_map/pallas_call | solution.py:427
Async XLA Ops:
  0.6 0.7 %copy-start = (s32[64]{0:T(128)S(1)}, s32[64]{0:T(128)}, u32[]{:S(2)}) copy-start(s32[64]{0:T(128)} %start_hbm.1) | copy-start | bytes 772
  1.3 0.7 %copy-start.1 = (s32[64]{0:T(128)S(1)}, s32[64]{0:T(128)}, u32[]{:S(2)}) copy-start(s32[64]{0:T(128)} %end_hbm.1) | copy-start | bytes 772

commit v2 on v1

--- a/solution.py
+++ b/solution.py
@@ -27,8 +27,8 @@
     n_s, n_t, rows, width, chunk,
     start_hbm, end_hbm, sig_hbm,
     smooth, slope, cov,
-    starts, stops, ext, wts, ends, res, mixed, halo, part, r1, mine, r2,
-    load_sem, bound_sem, halo_send, halo_recv, send_sem, recv_sem, s1_sem, s2_sem, met,
+    starts, stops, ext, wts, ends, res, mixed, halo, part, shares,
+    load_sem, bound_sem, halo_send, halo_recv, send_sem, recv_sem, share_sem, met,
 ):
     s = lax.axis_index("series")
     t = lax.axis_index("tm")
@@ -301,14 +301,22 @@
     for g in range(n_s):
         part[g] = pack(both[g * rows : (g + 1) * rows])
 
-    def first_stage(d):
-        peer = lax.rem(s + d, n_s)
+    here = t * n_s + s
+    peers = n_t * n_s - 1
+
+    def share(i):
+        peer = jnp.where(i < here, i, i + 1)
+        to_t, to_s = lax.div(peer, n_s), lax.rem(peer, n_s)
         return pltpu.make_async_remote_copy(
-            part.at[peer], r1.at[d - 1], s1_sem.at[0], s1_sem.at[1],
-            device_id={"series": peer}, device_id_type=MESH)
-
-    for d in range(1, n_s):
-        first_stage(d).start()
+            part.at[to_s], shares.at[here], share_sem.at[0], share_sem.at[1],
+            device_id={"tm": to_t, "series": to_s}, device_id_type=MESH)
+
+    def spread_shares(i, carry):
+        share(i).start()
+        return carry
+
+    lax.fori_loop(0, peers, spread_shares, 0)
+    shares[here] = part[s]
 
     lane = lax.broadcasted_iota(jnp.int32, (rows, 2 * total), 1)
     lane = jnp.where(lane < total, lane, lane - total)
@@ -319,24 +327,6 @@
         last_k = jnp.where(lane == i, stops[i], last_k)
     count = pack((jnp.minimum(last_k, last) - jnp.maximum(first_k, first)).astype(f32))
 
-    def gather(ref, sems):
-        return pltpu.make_async_remote_copy(
-            ref, ref, sems.at[0], sems.at[1], device_id={"series": lax.rem(s + 1, n_s)}, device_id_type=MESH)
-
-    own = part[s]
-    gather(r1, s1_sem).wait_recv()
-    for d in range(1, n_s):
-        own = own + r1[d - 1]
-    mine[...] = own
-
-    def second_stage(d):
-        return pltpu.make_async_remote_copy(
-            mine, r2.at[t], s2_sem.at[0], s2_sem.at[1],
-            device_id={"tm": lax.rem(t + d, n_t)}, device_id_type=MESH)
-
-    for d in range(1, n_t):
-        second_stage(d).start()
-    r2[t] = own
     sent = res.at[:, pl.ds(0, sends * chunk)]
     pltpu.make_async_remote_copy(
         sent, sent, send_sem, recv_sem.at[0],
@@ -350,15 +340,18 @@
     def _():
         to_left.wait_send()
 
-    gather(r1, s1_sem).wait_send()
-    gather(r2.at[pl.ds(0, n_t - 1)], s2_sem).wait_recv()
-    full = r2[0]
-    for d in range(1, n_t):
-        full = full + r2[d]
+    others = shares.at[pl.ds(0, peers)]
+    shared = pltpu.make_async_remote_copy(
+        others, others, share_sem.at[0], share_sem.at[1],
+        device_id={"series": lax.rem(s + 1, n_s)}, device_id_type=MESH)
+    shared.wait_recv()
+    full = shares[0]
+    for d in range(1, peers + 1):
+        full = full + shares[d]
     full = full / count
     cov[:half] = full[:, :total]
     cov[half:] = pltpu.roll(full, total, 1)[:, :total]
-    gather(r2.at[pl.ds(0, n_t - 1)], s2_sem).wait_send()
+    shared.wait_send()
 
 
 FLUSHES = 4
@@ -407,9 +400,7 @@
                 pltpu.VMEM((n_s, rows, quarter), f32),
                 pltpu.VMEM((2, rows, LANE), f32),
                 pltpu.VMEM((n_s, rows // 2, 2 * total), f32),
-                pltpu.VMEM((n_s - 1, rows // 2, 2 * total), f32),
-                pltpu.VMEM((rows // 2, 2 * total), f32),
-                pltpu.VMEM((n_t, rows // 2, 2 * total), f32),
+                pltpu.VMEM((n_t * n_s, rows // 2, 2 * total), f32),
                 dma((2,)),
                 dma((2,)),
                 dma((2,)),
@@ -417,13 +408,12 @@
                 dma,
                 dma((per,)),
                 dma((2,)),
-                dma((2,)),
                 pltpu.SemaphoreType.REGULAR((n_t.bit_length() + 1,)),
             ],
             compiler_params=pltpu.CompilerParams(
                 collective_id=0, has_side_effects=True, vmem_limit_bytes=67043328 - 8 * rows * width - 12 * 1024 * 1024
             ),
-        )(valid_start, valid_end, signal)
+        )(*[pltpu.with_memory_space_constraint(v, pltpu.HBM) for v in (valid_start, valid_end)], signal)
         return pl.pallas_call(
             flush,
             out_shape=tuple(jax.ShapeDtypeStruct(v.shape, f32) for v in kept),

time: 40.8 us -> 37.5 us (0.919)
  Pallas kernels: 38.6 us -> 36.7 us
  local copies, waits for them, and re-layouts: 1.3 us -> 0 us
    pallas_call x1, Pallas kernels: 36.6 us -> 34.6 us  [shards(): pl.pallas_call(functools.partial(kernel, n_s, n_t, rows, width, chunk), o...]
    unnamed x4 -> x0, local copies, waits for them, and re-layouts: 1.3 us -> none
where the time goes in v2:
time: 37.5 us; the launch traced here: 37.3 us
  Pallas kernels  36.7 us (98%)
  between operations  0.64 us (2%)
    pallas_call x1, Pallas kernels, shards(): pl.pallas_call(functools.partial(kernel, n_s, n_t, rows, width, chunk), o...  34.6 us
    pallas_call x1, Pallas kernels, shards(): pl.pallas_call(flush, out_shape=tuple((jax.ShapeDtypeStruct(v.shape, f32)...  2.09 us

profile of v2, /device:TPU:0, one launch (start us, length us, event | category | flops | bytes accessed | tf_op | source)
XLA Modules:
  0.0 37.3 jit_solution(8177683203575712588)
XLA Ops:
  0.6 34.6 %shard_map.58 = (f32[16,32768]{1,0:T(8,128)S(1)}, f32[16,32768]{1,0:T(8,128)S(1)}, f32[16,64]{1,0:T(8,128)S(1)}) custom-call(s32[64]{0:T(128)} %start_hbm.1, s32[64]{0:T(128)} %end_hbm.1, f32[16,32768]{1,0:T(8,128)} %sig_hbm.1), custom_call_target="tpu_custom_call" | custom-call | tf_op jit(solution)/shard_map/pallas_call | solution.py:384
  35.3 2.1 %shard_map.59 = (f32[16,32768]{1,0:T(8,128)}, f32[16,32768]{1,0:T(8,128)}, f32[16,64]{1,0:T(8,128)}) custom-call(f32[16,32768]{1,0:T(8,128)S(1)} %get-tuple-element.6.smooth, f32[16,32768]{1,0:T(8,128)S(1)} %get-tuple-element.7.slope, f32[16,64]{1,0:T(8,128)S(1)} %get-tuple-element.8.cov), custom_call_target="tpu_custom_call" | custom-call | tf_op jit(solution)/shard_map/pallas_call | solution.py:417

commit v3 on v2

--- a/solution.py
+++ b/solution.py
@@ -27,8 +27,8 @@
     n_s, n_t, rows, width, chunk,
     start_hbm, end_hbm, sig_hbm,
     smooth, slope, cov,
-    starts, stops, ext, wts, ends, res, mixed, halo, part, shares,
-    load_sem, bound_sem, halo_send, halo_recv, send_sem, recv_sem, share_sem, met,
+    starts, stops, ext, wts, ends, res, mixed, halo, part, shares, relay,
+    load_sem, bound_sem, halo_send, halo_recv, send_sem, recv_sem, share_sem, met, relay_send, relay_recv,
 ):
     s = lax.axis_index("series")
     t = lax.axis_index("tm")
@@ -39,6 +39,14 @@
     total = n_s * rows
     tiles = chunk // LANE
     group = 2 - n_t % 2
+    pairs = n_t // group
+    rounds = []
+    far = 2 * group
+    while far < n_t:
+        rounds.append(far)
+        far *= 2
+    rounds.append(0)
+    swaps = n_s == 4 and len(rounds) > 1 and per >= 8
     f32 = jnp.float32
 
     def offset(qi):
@@ -145,6 +153,13 @@
         device_id={"tm": left}, device_id_type=MESH)
     has_right, has_left = t < n_t - 1, t > 0
 
+    mirror = t + group * (pairs - 1 - 2 * lax.div(t, group))
+    gap = lax.div(t - mirror, group)
+    whole_from, whole_to = gap == 3, gap == -3
+    half_from, half_to = gap == 1, gap == -1
+    detour = per + 2
+    across = lax.rem(s + offset(1), n_s)
+
     def place(k):
         qi = k // per
         q = lax.rem(s + offset(qi), n_s)
@@ -158,6 +173,50 @@
             mixed.at[s, :, pl.ds(pl.multiple_of(j * chunk, chunk), chunk)],
             send_sem, recv_sem.at[j],
             device_id={"series": q}, device_id_type=MESH)
+
+    def column(j):
+        return pl.multiple_of(j * chunk, chunk)
+
+    def away(k, n):
+        q, j = place(k)
+        size = chunk if n == 0 else chunk // 2
+        return pltpu.make_async_remote_copy(
+            res.at[:, pl.ds(column(q * per + j), size)], relay.at[n, :, pl.ds(0, size)],
+            send_sem, relay_recv.at[n],
+            device_id={"series": across, "tm": mirror}, device_id_type=MESH)
+
+    def onward(n):
+        j = detour + n - per + 1
+        size = chunk if n == 0 else chunk // 2
+        return pltpu.make_async_remote_copy(
+            relay.at[n, :, pl.ds(0, size)], mixed.at[across, :, pl.ds(j * chunk, size)],
+            relay_send.at[n], recv_sem.at[j],
+            device_id={"tm": mirror}, device_id_type=MESH)
+
+    def rest(k):
+        q, j = place(k)
+        at = chunk // 2
+        return pltpu.make_async_remote_copy(
+            res.at[:, pl.ds(column(q * per + j) + at, at)],
+            mixed.at[s, :, pl.ds(column(j) + at, at)],
+            send_sem, recv_sem.at[j],
+            device_id={"series": q}, device_id_type=MESH)
+
+    def greeting(i):
+        if i > len(rounds):
+            return
+        if i > 0:
+            far = rounds[i - 1]
+            if far:
+                pl.semaphore_wait(met.at[i], heard(far))
+            elif group == 2:
+                pl.semaphore_wait(met.at[i], 1)
+        if i < len(rounds):
+            far = rounds[i]
+            if far:
+                reach(met.at[i + 1], far)
+            elif group == 2:
+                tell(met.at[i + 1], partner)
 
     def spread(v):
         return jnp.concatenate([v] * tiles, axis=1)
@@ -239,36 +298,43 @@
             def _():
                 to_left.start()
 
-        @pl.when((k >= 1) & (k <= sends))
+            greeting(0)
+
+        @pl.when(k == max(detour, greet + 1))
+        def _():
+            greeting(1)
+
+        direct = (k >= 1) & (k <= sends)
+        if swaps:
+            direct &= jnp.logical_not(((k == detour + 1) & whole_from) | ((k == detour + 2) & half_from))
+
+        @pl.when(direct)
         def _():
             transfer(k - 1).start()
 
+        if swaps:
+            @pl.when((k == detour + 1) & whole_from)
+            def _():
+                away(k - 1, 0).start()
+
+            @pl.when((k == detour + 2) & half_from)
+            def _():
+                away(k - 1, 1).start()
+                rest(k - 1).start()
+
         return carry
 
     lax.fori_loop(0, steps, step, 0)
 
-    rounds = []
-    far = 2 * group
-    while far < n_t:
-        rounds.append(far)
-        far *= 2
-    rounds.append(0)
-
-    def greeting(i):
-        if i > len(rounds):
-            return
-        if i > 0:
-            far = rounds[i - 1]
-            if far:
-                pl.semaphore_wait(met.at[i], heard(far))
-            elif group == 2:
-                pl.semaphore_wait(met.at[i], 1)
-        if i < len(rounds):
-            far = rounds[i]
-            if far:
-                reach(met.at[i + 1], far)
-            elif group == 2:
-                tell(met.at[i + 1], partner)
+    def pass_on(n):
+        def move():
+            away(detour + n, n).wait_recv()
+            onward(n).start()
+        return move
+
+    if swaps:
+        pl.when(whole_to)(pass_on(0))
+        pl.when(half_to)(pass_on(1))
 
     def arrival(i):
         j = (i + 1) % per
@@ -285,7 +351,7 @@
 
     gram = jnp.zeros((2 * total, 2 * total), f32)
     for i in range(per):
-        greeting(i)
+        greeting(i + 2)
         arrival(i).wait_recv()
         j = (i + 1) % per
         x = jnp.concatenate(
@@ -294,7 +360,7 @@
         lo = (x - hi.astype(f32)).astype(jnp.bfloat16)
         z = jnp.concatenate([hi, lo], axis=0)
         gram = gram + lax.dot_general(z, z, (((1,), (1,)), ((), ())), preferred_element_type=f32)
-    for i in range(per, len(rounds) + 1):
+    for i in range(per + 2, len(rounds) + 1):
         greeting(i)
     both = gram[:total] + gram[total:]
     both = both + pltpu.roll(both, total, 1)
@@ -303,10 +369,12 @@
 
     here = t * n_s + s
     peers = n_t * n_s - 1
+    turn = (lax.rem(t, group) * pairs + lax.div(t, group)) * n_s + s
 
     def share(i):
-        peer = jnp.where(i < here, i, i + 1)
-        to_t, to_s = lax.div(peer, n_s), lax.rem(peer, n_s)
+        i = jnp.where(i < turn, i, i + 1)
+        row_of, to_s = lax.div(i, n_s), lax.rem(i, n_s)
+        to_t = lax.rem(row_of, pairs) * group + lax.div(row_of, pairs)
         return pltpu.make_async_remote_copy(
             part.at[to_s], shares.at[here], share_sem.at[0], share_sem.at[1],
             device_id={"tm": to_t, "series": to_s}, device_id_type=MESH)
@@ -340,6 +408,9 @@
     def _():
         to_left.wait_send()
 
+    if swaps:
+        pl.when(whole_to)(onward(0).wait_send)
+        pl.when(half_to)(onward(1).wait_send)
     others = shares.at[pl.ds(0, peers)]
     shared = pltpu.make_async_remote_copy(
         others, others, share_sem.at[0], share_sem.at[1],
@@ -401,6 +472,7 @@
                 pltpu.VMEM((2, rows, LANE), f32),
                 pltpu.VMEM((n_s, rows // 2, 2 * total), f32),
                 pltpu.VMEM((n_t * n_s, rows // 2, 2 * total), f32),
+                pltpu.VMEM((2, rows, chunk), f32),
                 dma((2,)),
                 dma((2,)),
                 dma((2,)),
@@ -409,6 +481,8 @@
                 dma((per,)),
                 dma((2,)),
                 pltpu.SemaphoreType.REGULAR((n_t.bit_length() + 1,)),
+                dma((2,)),
+                dma((2,)),
             ],
             compiler_params=pltpu.CompilerParams(
                 collective_id=0, has_side_effects=True, vmem_limit_bytes=67043328 - 8 * rows * width - 12 * 1024 * 1024

time: 37.5 us -> 36.4 us (0.971)
  Pallas kernels: 36.7 us -> 35.6 us
    pallas_call x1, Pallas kernels: 34.6 us -> 33.5 us  [shards(): pl.pallas_call(functools.partial(kernel, n_s, n_t, rows, width, chunk), o...]
where the time goes in v3:
time: 36.4 us; the launch traced here: 36.3 us
  Pallas kernels  35.6 us (98%)
  between operations  0.64 us (2%)
    pallas_call x1, Pallas kernels, shards(): pl.pallas_call(functools.partial(kernel, n_s, n_t, rows, width, chunk), o...  33.5 us
    pallas_call x1, Pallas kernels, shards(): pl.pallas_call(flush, out_shape=tuple((jax.ShapeDtypeStruct(v.shape, f32)...  2.09 us

profile of v3, /device:TPU:0, one launch (start us, length us, event | category | flops | bytes accessed | tf_op | source)
XLA Modules:
  0.0 36.3 jit_solution(2517602884717627545)
XLA Ops:
  0.6 33.5 %shard_map.58 = (f32[16,32768]{1,0:T(8,128)S(1)}, f32[16,32768]{1,0:T(8,128)S(1)}, f32[16,64]{1,0:T(8,128)S(1)}) custom-call(s32[64]{0:T(128)} %start_hbm.1, s32[64]{0:T(128)} %end_hbm.1, f32[16,32768]{1,0:T(8,128)} %sig_hbm.1), custom_call_target="tpu_custom_call" | custom-call | tf_op jit(solution)/shard_map/pallas_call | solution.py:455
  34.2 2.1 %shard_map.59 = (f32[16,32768]{1,0:T(8,128)}, f32[16,32768]{1,0:T(8,128)}, f32[16,64]{1,0:T(8,128)}) custom-call(f32[16,32768]{1,0:T(8,128)S(1)} %get-tuple-element.6.smooth, f32[16,32768]{1,0:T(8,128)S(1)} %get-tuple-element.7.slope, f32[16,64]{1,0:T(8,128)S(1)} %get-tuple-element.8.cov), custom_call_target="tpu_custom_call" | custom-call | tf_op jit(solution)/shard_map/pallas_call | solution.py:491

commit v4 on v3

--- a/solution.py
+++ b/solution.py
@@ -26,8 +26,8 @@
 def kernel(
     n_s, n_t, rows, width, chunk,
     start_hbm, end_hbm, sig_hbm,
-    smooth, slope, cov,
-    starts, stops, ext, wts, ends, res, mixed, halo, part, shares, relay,
+    smooth, slope, shares, count,
+    starts, stops, ext, wts, ends, res, mixed, halo, part, relay,
     load_sem, bound_sem, halo_send, halo_recv, send_sem, recv_sem, share_sem, met, relay_send, relay_recv,
 ):
     s = lax.axis_index("series")
@@ -46,7 +46,7 @@
         rounds.append(far)
         far *= 2
     rounds.append(0)
-    swaps = n_s == 4 and len(rounds) > 1 and per >= 8
+    swaps = n_s == 4 and group == 2 and len(rounds) > 1 and per >= 8
     f32 = jnp.float32
 
     def offset(qi):
@@ -157,7 +157,9 @@
     gap = lax.div(t - mirror, group)
     whole_from, whole_to = gap == 3, gap == -3
     half_from, half_to = gap == 1, gap == -1
+    side_from, side_to = lax.rem(t, 2) == 1, lax.rem(t, 2) == 0
     detour = per + 2
+    lag = per
     across = lax.rem(s + offset(1), n_s)
 
     def place(k):
@@ -192,6 +194,20 @@
             relay.at[n, :, pl.ds(0, size)], mixed.at[across, :, pl.ds(j * chunk, size)],
             relay_send.at[n], recv_sem.at[j],
             device_id={"tm": mirror}, device_id_type=MESH)
+
+    def aside():
+        q, j = place(detour - 1)
+        return pltpu.make_async_remote_copy(
+            res.at[:, pl.ds(column(q * per + j), chunk // 2)], relay.at[2, :, pl.ds(0, chunk // 2)],
+            send_sem, relay_recv.at[2],
+            device_id={"tm": partner}, device_id_type=MESH)
+
+    def over():
+        j = detour - per
+        return pltpu.make_async_remote_copy(
+            relay.at[2, :, pl.ds(0, chunk // 2)], mixed.at[s, :, pl.ds(j * chunk, chunk // 2)],
+            relay_send.at[2], recv_sem.at[j],
+            device_id={"series": across, "tm": partner}, device_id_type=MESH)
 
     def rest(k):
         q, j = place(k)
@@ -304,23 +320,41 @@
         def _():
             greeting(1)
 
-        direct = (k >= 1) & (k <= sends)
-        if swaps:
-            direct &= jnp.logical_not(((k == detour + 1) & whole_from) | ((k == detour + 2) & half_from))
-
-        @pl.when(direct)
-        def _():
-            transfer(k - 1).start()
-
-        if swaps:
-            @pl.when((k == detour + 1) & whole_from)
+        if not swaps:
+            @pl.when((k >= 1) & (k <= sends))
             def _():
-                away(k - 1, 0).start()
-
-            @pl.when((k == detour + 2) & half_from)
-            def _():
-                away(k - 1, 1).start()
-                rest(k - 1).start()
+                transfer(k - 1).start()
+
+            return carry
+
+        @pl.when((k == detour) & side_from)
+        def _():
+            aside().start()
+
+        @pl.when((k == detour + 1) & whole_from)
+        def _():
+            away(k - 1, 0).start()
+
+        @pl.when((k == detour + 2) & half_from)
+        def _():
+            away(k - 1, 1).start()
+
+        @pl.when((k == per + lag) & side_to)
+        def _():
+            aside().wait_recv()
+            over().start()
+
+        m = jnp.where(k <= per, k - 1, k - 1 - lag)
+        split = ((m == detour - 1) & side_from) | ((m == detour + 1) & half_from)
+        ready = ((k >= 1) & (k <= per)) | ((k > per + lag) & (m < sends))
+
+        @pl.when(ready & jnp.logical_not(split | ((m == detour) & whole_from)))
+        def _():
+            transfer(m).start()
+
+        @pl.when(ready & split)
+        def _():
+            rest(m).start()
 
         return carry
 
@@ -333,6 +367,8 @@
         return move
 
     if swaps:
+        for m in range(steps - 1 - lag, sends):
+            transfer(m).start()
         pl.when(whole_to)(pass_on(0))
         pl.when(half_to)(pass_on(1))
 
@@ -369,21 +405,24 @@
 
     here = t * n_s + s
     peers = n_t * n_s - 1
-    turn = (lax.rem(t, group) * pairs + lax.div(t, group)) * n_s + s
-
-    def share(i):
-        i = jnp.where(i < turn, i, i + 1)
-        row_of, to_s = lax.div(i, n_s), lax.rem(i, n_s)
-        to_t = lax.rem(row_of, pairs) * group + lax.div(row_of, pairs)
+
+    def share(to_t, to_s):
         return pltpu.make_async_remote_copy(
             part.at[to_s], shares.at[here], share_sem.at[0], share_sem.at[1],
             device_id={"tm": to_t, "series": to_s}, device_id_type=MESH)
 
     def spread_shares(i, carry):
-        share(i).start()
+        beyond = i - group
+        beyond = (1 + lax.rem(beyond, pairs - 1)) * group + lax.div(beyond, pairs - 1)
+        to_t = jnp.where(i < group, i, beyond)
+        for to_s in range(n_s):
+            @pl.when((to_t != t) | (s != to_s))
+            def _():
+                share(to_t, to_s).start()
+
         return carry
 
-    lax.fori_loop(0, peers, spread_shares, 0)
+    lax.fori_loop(0, n_t, spread_shares, 0)
     shares[here] = part[s]
 
     lane = lax.broadcasted_iota(jnp.int32, (rows, 2 * total), 1)
@@ -393,7 +432,7 @@
     for i in range(total):
         first_k = jnp.where(lane == i, starts[i], first_k)
         last_k = jnp.where(lane == i, stops[i], last_k)
-    count = pack((jnp.minimum(last_k, last) - jnp.maximum(first_k, first)).astype(f32))
+    count[...] = pack((jnp.minimum(last_k, last) - jnp.maximum(first_k, first)).astype(f32))
 
     sent = res.at[:, pl.ds(0, sends * chunk)]
     pltpu.make_async_remote_copy(
@@ -411,32 +450,37 @@
     if swaps:
         pl.when(whole_to)(onward(0).wait_send)
         pl.when(half_to)(onward(1).wait_send)
+        pl.when(side_to)(over().wait_send)
     others = shares.at[pl.ds(0, peers)]
     shared = pltpu.make_async_remote_copy(
         others, others, share_sem.at[0], share_sem.at[1],
         device_id={"series": lax.rem(s + 1, n_s)}, device_id_type=MESH)
     shared.wait_recv()
-    full = shares[0]
-    for d in range(1, peers + 1):
-        full = full + shares[d]
-    full = full / count
-    cov[:half] = full[:, :total]
-    cov[half:] = pltpu.roll(full, total, 1)[:, :total]
     shared.wait_send()
 
 
-FLUSHES = 4
-
-
-def flush(smooth, slope, cov, smooth_out, slope_out, cov_out, sems, cov_sem):
+FLUSHES = 1
+
+
+def flush(smooth, slope, shares, count, smooth_out, slope_out, cov_out, cov, sems, cov_sem):
     piece = smooth.shape[1] // FLUSHES
-    copies = [pltpu.make_async_copy(cov, cov_out, cov_sem)]
+    copies = []
     for i in range(FLUSHES):
         span = pl.ds(i * piece, piece)
         copies.append(pltpu.make_async_copy(smooth.at[:, span], smooth_out.at[:, span], sems.at[2 * i]))
         copies.append(pltpu.make_async_copy(slope.at[:, span], slope_out.at[:, span], sems.at[2 * i + 1]))
     for copy in copies:
         copy.start()
+    full = shares[0]
+    for d in range(1, shares.shape[0]):
+        full = full + shares[d]
+    full = full / count[...]
+    half, total = full.shape[0], full.shape[1] // 2
+    cov[:half] = full[:, :total]
+    cov[half:] = pltpu.roll(full, total, 1)[:, :total]
+    last = pltpu.make_async_copy(cov, cov_out, cov_sem)
+    last.start()
+    copies.append(last)
     for copy in copies:
         copy.wait()
 
@@ -457,10 +501,11 @@
             out_shape=(
                 jax.ShapeDtypeStruct((rows, width), f32),
                 jax.ShapeDtypeStruct((rows, width), f32),
-                jax.ShapeDtypeStruct((rows, total), f32),
+                jax.ShapeDtypeStruct((n_t * n_s, rows // 2, 2 * total), f32),
+                jax.ShapeDtypeStruct((rows // 2, 2 * total), f32),
             ),
             in_specs=[pl.BlockSpec(memory_space=pltpu.HBM)] * 3,
-            out_specs=(pl.BlockSpec(memory_space=pltpu.VMEM),) * 3,
+            out_specs=(pl.BlockSpec(memory_space=pltpu.VMEM),) * 4,
             scratch_shapes=[
                 pltpu.SMEM((total,), jnp.int32),
                 pltpu.SMEM((total,), jnp.int32),
@@ -471,8 +516,7 @@
                 pltpu.VMEM((n_s, rows, quarter), f32),
                 pltpu.VMEM((2, rows, LANE), f32),
                 pltpu.VMEM((n_s, rows // 2, 2 * total), f32),
-                pltpu.VMEM((n_t * n_s, rows // 2, 2 * total), f32),
-                pltpu.VMEM((2, rows, chunk), f32),
+                pltpu.VMEM((3, rows, chunk), f32),
                 dma((2,)),
                 dma((2,)),
                 dma((2,)),
@@ -480,9 +524,9 @@
                 dma,
                 dma((per,)),
                 dma((2,)),
-                pltpu.SemaphoreType.REGULAR((n_t.bit_length() + 1,)),
-                dma((2,)),
-                dma((2,)),
+                pltpu.SemaphoreType.REGULAR((max(n_t.bit_length() - 1, 3),)),
+                dma((3,)),
+                dma((3,)),
             ],
             compiler_params=pltpu.CompilerParams(
                 collective_id=0, has_side_effects=True, vmem_limit_bytes=67043328 - 8 * rows * width - 12 * 1024 * 1024
@@ -490,10 +534,10 @@
         )(*[pltpu.with_memory_space_constraint(v, pltpu.HBM) for v in (valid_start, valid_end)], signal)
         return pl.pallas_call(
             flush,
-            out_shape=tuple(jax.ShapeDtypeStruct(v.shape, f32) for v in kept),
-            in_specs=[pl.BlockSpec(memory_space=pltpu.VMEM)] * 3,
+            out_shape=tuple(jax.ShapeDtypeStruct(v, f32) for v in ((rows, width), (rows, width), (rows, total))),
+            in_specs=[pl.BlockSpec(memory_space=pltpu.VMEM)] * 4,
             out_specs=(pl.BlockSpec(memory_space=pltpu.HBM),) * 3,
-            scratch_shapes=[dma((2 * FLUSHES,)), dma],
+            scratch_shapes=[pltpu.VMEM((rows, total), f32), dma((2 * FLUSHES,)), dma],
             compiler_params=pltpu.CompilerParams(vmem_limit_bytes=1024 * 1024),
         )(*kept)
 

time: 36.4 us -> 36.1 us (level)
  no operation moved by 1% of the time
where the time goes in v4:
time: 36.1 us; the launch traced here: 35.9 us
  Pallas kernels  35.3 us (98%)
  between operations  0.64 us (2%)
    pallas_call x1, Pallas kernels, shards(): pl.pallas_call(functools.partial(kernel, n_s, n_t, rows, width, chunk), o...  33.3 us
    pallas_call x1, Pallas kernels, shards(): pl.pallas_call(flush, out_shape=tuple((jax.ShapeDtypeStruct(v, f32) for v...  2.04 us

profile of v4, /device:TPU:0, one launch (start us, length us, event | category | flops | bytes accessed | tf_op | source)
XLA Modules:
  0.0 35.9 jit_solution(4143284270853981817)
XLA Ops:
  0.6 33.3 %shard_map.58 = (f32[16,32768]{1,0:T(8,128)S(1)}, f32[16,32768]{1,0:T(8,128)S(1)}, f32[32,8,128]{2,1,0:T(8,128)S(1)}, f32[8,128]{1,0:T(8,128)S(1)}) custom-call(s32[64]{0:T(128)} %start_hbm.1, s32[64]{0:T(128)} %end_hbm.1, f32[16,32768]{1,0:T(8,128)} %sig_hbm.1), custom_call_target="tpu_custom_call" | custom-call | tf_op jit(solution)/shard_map/pallas_call | solution.py:499
  33.9 2.0 %shard_map.59 = (f32[16,32768]{1,0:T(8,128)}, f32[16,32768]{1,0:T(8,128)}, f32[16,64]{1,0:T(8,128)}) custom-call(f32[16,32768]{1,0:T(8,128)S(1)} %get-tuple-element.7.smooth, f32[16,32768]{1,0:T(8,128)S(1)} %get-tuple-element.8.slope, f32[32,8,128]{2,1,0:T(8,128)S(1)} %get-tuple-element.9.shares, f32[8,128]{1,0:T(8,128)S(1)} %get-tuple-element.10.count), custom_call_target="tpu_custom_call" | custom-call | tf_op jit(solution)/shard_map/pallas_call | solution.py:535

commit v5 on v4

--- a/solution.py
+++ b/solution.py
@@ -23,11 +23,20 @@
     return chunk
 
 
+def rounds_of(n_t):
+    far = 2 * (2 - n_t % 2)
+    rounds = []
+    while far < n_t:
+        rounds.append(far)
+        far *= 2
+    return rounds
+
+
 def kernel(
     n_s, n_t, rows, width, chunk,
     start_hbm, end_hbm, sig_hbm,
     smooth, slope, shares, count,
-    starts, stops, ext, wts, ends, res, mixed, halo, part, relay,
+    starts, stops, ext, wts, ends, res, mixed, halo, part, summed, relay,
     load_sem, bound_sem, halo_send, halo_recv, send_sem, recv_sem, share_sem, met, relay_send, relay_recv,
 ):
     s = lax.axis_index("series")
@@ -40,13 +49,8 @@
     tiles = chunk // LANE
     group = 2 - n_t % 2
     pairs = n_t // group
-    rounds = []
-    far = 2 * group
-    while far < n_t:
-        rounds.append(far)
-        far *= 2
-    rounds.append(0)
-    swaps = n_s == 4 and group == 2 and len(rounds) > 1 and per >= 8
+    rounds = rounds_of(n_t)
+    swaps = n_s == 4 and group == 2 and rounds and per >= 8
     f32 = jnp.float32
 
     def offset(qi):
@@ -160,6 +164,7 @@
     side_from, side_to = lax.rem(t, 2) == 1, lax.rem(t, 2) == 0
     detour = per + 2
     lag = per
+    slip = 3 * chunk // 8
     across = lax.rem(s + offset(1), n_s)
 
     def place(k):
@@ -183,56 +188,45 @@
         q, j = place(k)
         size = chunk if n == 0 else chunk // 2
         return pltpu.make_async_remote_copy(
-            res.at[:, pl.ds(column(q * per + j), size)], relay.at[n, :, pl.ds(0, size)],
-            send_sem, relay_recv.at[n],
+            res.at[:, pl.ds(column(q * per + j), size)], relay.at[0, :, pl.ds(0, size)],
+            send_sem, relay_recv.at[0],
             device_id={"series": across, "tm": mirror}, device_id_type=MESH)
 
     def onward(n):
         j = detour + n - per + 1
         size = chunk if n == 0 else chunk // 2
         return pltpu.make_async_remote_copy(
-            relay.at[n, :, pl.ds(0, size)], mixed.at[across, :, pl.ds(j * chunk, size)],
-            relay_send.at[n], recv_sem.at[j],
+            relay.at[0, :, pl.ds(0, size)], mixed.at[across, :, pl.ds(j * chunk, size)],
+            relay_send.at[0], recv_sem.at[j],
             device_id={"tm": mirror}, device_id_type=MESH)
 
     def aside():
         q, j = place(detour - 1)
         return pltpu.make_async_remote_copy(
-            res.at[:, pl.ds(column(q * per + j), chunk // 2)], relay.at[2, :, pl.ds(0, chunk // 2)],
-            send_sem, relay_recv.at[2],
+            res.at[:, pl.ds(column(q * per + j), slip)], relay.at[1, :, pl.ds(0, slip)],
+            send_sem, relay_recv.at[1],
             device_id={"tm": partner}, device_id_type=MESH)
 
     def over():
         j = detour - per
         return pltpu.make_async_remote_copy(
-            relay.at[2, :, pl.ds(0, chunk // 2)], mixed.at[s, :, pl.ds(j * chunk, chunk // 2)],
-            relay_send.at[2], recv_sem.at[j],
+            relay.at[1, :, pl.ds(0, slip)], mixed.at[s, :, pl.ds(j * chunk, slip)],
+            relay_send.at[1], recv_sem.at[j],
             device_id={"series": across, "tm": partner}, device_id_type=MESH)
 
-    def rest(k):
+    def rest(k, at):
         q, j = place(k)
-        at = chunk // 2
-        return pltpu.make_async_remote_copy(
-            res.at[:, pl.ds(column(q * per + j) + at, at)],
-            mixed.at[s, :, pl.ds(column(j) + at, at)],
+        return pltpu.make_async_remote_copy(
+            res.at[:, pl.ds(column(q * per + j) + at, chunk - at)],
+            mixed.at[s, :, pl.ds(column(j) + at, chunk - at)],
             send_sem, recv_sem.at[j],
             device_id={"series": q}, device_id_type=MESH)
 
     def greeting(i):
-        if i > len(rounds):
-            return
-        if i > 0:
-            far = rounds[i - 1]
-            if far:
-                pl.semaphore_wait(met.at[i], heard(far))
-            elif group == 2:
-                pl.semaphore_wait(met.at[i], 1)
+        if 0 < i <= len(rounds):
+            pl.semaphore_wait(met.at[i], heard(rounds[i - 1]))
         if i < len(rounds):
-            far = rounds[i]
-            if far:
-                reach(met.at[i + 1], far)
-            elif group == 2:
-                tell(met.at[i + 1], partner)
+            reach(met.at[i + 1], rounds[i])
 
     def spread(v):
         return jnp.concatenate([v] * tiles, axis=1)
@@ -345,16 +339,20 @@
             over().start()
 
         m = jnp.where(k <= per, k - 1, k - 1 - lag)
-        split = ((m == detour - 1) & side_from) | ((m == detour + 1) & half_from)
+        fork, split = (m == detour - 1) & side_from, (m == detour + 1) & half_from
         ready = ((k >= 1) & (k <= per)) | ((k > per + lag) & (m < sends))
 
-        @pl.when(ready & jnp.logical_not(split | ((m == detour) & whole_from)))
+        @pl.when(ready & jnp.logical_not(fork | split | ((m == detour) & whole_from)))
         def _():
             transfer(m).start()
 
+        @pl.when(ready & fork)
+        def _():
+            rest(m, slip).start()
+
         @pl.when(ready & split)
         def _():
-            rest(m).start()
+            rest(m, chunk // 2).start()
 
         return carry
 
@@ -400,30 +398,68 @@
         greeting(i)
     both = gram[:total] + gram[total:]
     both = both + pltpu.roll(both, total, 1)
+    here = t * n_s + s
+    whole = n_t * n_s
+    nest = n_t * n_s // 2
+    first_in = (t == 0) & (s < 2)
+
+    def early(to_s):
+        return pltpu.make_async_remote_copy(
+            part.at[to_s], shares.at[here], share_sem.at[0], share_sem.at[1],
+            device_id={"tm": 0, "series": to_s}, device_id_type=MESH)
+
     for g in range(n_s):
         part[g] = pack(both[g * rows : (g + 1) * rows])
-
-    here = t * n_s + s
-    peers = n_t * n_s - 1
-
-    def share(to_t, to_s):
-        return pltpu.make_async_remote_copy(
-            part.at[to_s], shares.at[here], share_sem.at[0], share_sem.at[1],
-            device_id={"tm": to_t, "series": to_s}, device_id_type=MESH)
+        if g < 2:
+            @pl.when((t != 0) | (s != g))
+            def _():
+                early(g).start()
+
+
+    core = lax.rem(s, 2)
+    mate = s + 1 - 2 * core
+
+    def swap(g):
+        return pltpu.make_async_remote_copy(
+            part.at[g * 2 + 1 - core], summed.at[n_s // 2 + g], load_sem.at[0], load_sem.at[1],
+            device_id={"series": mate}, device_id_type=MESH)
+
+    for g in range(n_s // 2):
+        swap(g).start()
+    got = summed.at[pl.ds(n_s // 2, n_s // 2)]
+    both_swaps = pltpu.make_async_remote_copy(
+        got, got, load_sem.at[0], load_sem.at[1], device_id={"series": mate}, device_id_type=MESH)
+    both_swaps.wait_recv()
+    for g in range(n_s // 2):
+        summed[g] = part[g * 2 + core] + summed[n_s // 2 + g]
+
+    def share(to_t, to_x):
+        return pltpu.make_async_remote_copy(
+            summed.at[to_x], shares.at[t * (n_s // 2) + lax.div(s, 2)], share_sem.at[0], share_sem.at[1],
+            device_id={"tm": to_t, "series": to_x * 2 + core}, device_id_type=MESH)
 
     def spread_shares(i, carry):
         beyond = i - group
         beyond = (1 + lax.rem(beyond, pairs - 1)) * group + lax.div(beyond, pairs - 1)
         to_t = jnp.where(i < group, i, beyond)
-        for to_s in range(n_s):
-            @pl.when((to_t != t) | (s != to_s))
-            def _():
-                share(to_t, to_s).start()
+        for to_x in range(n_s // 2):
+            @pl.when(((to_t != t) | (lax.div(s, 2) != to_x)) & ((to_t != 0) | (to_x != 0)))
+            def _():
+                share(to_t, to_x).start()
 
         return carry
 
     lax.fori_loop(0, n_t, spread_shares, 0)
-    shares[here] = part[s]
+    both_swaps.wait_send()
+
+    @pl.when(first_in)
+    def _():
+        shares[here] = part[s]
+
+    @pl.when(jnp.logical_not(first_in))
+    def _():
+        shares[t * (n_s // 2) + lax.div(s, 2)] = summed[lax.div(s, 2)]
+        shares[nest:] = jnp.zeros((whole - nest, half, 2 * total), f32)
 
     lane = lax.broadcasted_iota(jnp.int32, (rows, 2 * total), 1)
     lane = jnp.where(lane < total, lane, lane - total)
@@ -451,12 +487,15 @@
         pl.when(whole_to)(onward(0).wait_send)
         pl.when(half_to)(onward(1).wait_send)
         pl.when(side_to)(over().wait_send)
-    others = shares.at[pl.ds(0, peers)]
-    shared = pltpu.make_async_remote_copy(
-        others, others, share_sem.at[0], share_sem.at[1],
-        device_id={"series": lax.rem(s + 1, n_s)}, device_id_type=MESH)
-    shared.wait_recv()
-    shared.wait_send()
+    def batch(n):
+        block = shares.at[pl.ds(0, n)]
+        return pltpu.make_async_remote_copy(
+            block, block, share_sem.at[0], share_sem.at[1],
+            device_id={"series": lax.rem(s + 1, n_s)}, device_id_type=MESH)
+
+    pl.when(first_in)(batch(whole - 1).wait_recv)
+    pl.when(jnp.logical_not(first_in))(batch(nest - 1).wait_recv)
+    batch(nest).wait_send()
 
 
 FLUSHES = 1
@@ -516,7 +555,8 @@
                 pltpu.VMEM((n_s, rows, quarter), f32),
                 pltpu.VMEM((2, rows, LANE), f32),
                 pltpu.VMEM((n_s, rows // 2, 2 * total), f32),
-                pltpu.VMEM((3, rows, chunk), f32),
+                pltpu.VMEM((n_s, rows // 2, 2 * total), f32),
+                pltpu.VMEM((2, rows, chunk), f32),
                 dma((2,)),
                 dma((2,)),
                 dma((2,)),
@@ -524,9 +564,9 @@
                 dma,
                 dma((per,)),
                 dma((2,)),
-                pltpu.SemaphoreType.REGULAR((max(n_t.bit_length() - 1, 3),)),
-                dma((3,)),
-                dma((3,)),
+                pltpu.SemaphoreType.REGULAR((1 + len(rounds_of(n_t)),)),
+                dma((2,)),
+                dma((2,)),
             ],
             compiler_params=pltpu.CompilerParams(
                 collective_id=0, has_side_effects=True, vmem_limit_bytes=67043328 - 8 * rows * width - 12 * 1024 * 1024

time: 36.1 us -> 35.8 us (level)
  no operation moved by 1% of the time
where the time goes in v5:
time: 35.8 us; the launch traced here: 35.6 us
  Pallas kernels  35 us (98%)
  between operations  0.64 us (2%)
    pallas_call x1, Pallas kernels, shards(): pl.pallas_call(functools.partial(kernel, n_s, n_t, rows, width, chunk), o...  32.9 us
    pallas_call x1, Pallas kernels, shards(): pl.pallas_call(flush, out_shape=tuple((jax.ShapeDtypeStruct(v, f32) for v...  2.04 us

profile of v5, /device:TPU:0, one launch (start us, length us, event | category | flops | bytes accessed | tf_op | source)
XLA Modules:
  0.0 35.6 jit_solution(6593319100679188502)
XLA Ops:
  0.6 32.9 %shard_map.58 = (f32[16,32768]{1,0:T(8,128)S(1)}, f32[16,32768]{1,0:T(8,128)S(1)}, f32[32,8,128]{2,1,0:T(8,128)S(1)}, f32[8,128]{1,0:T(8,128)S(1)}) custom-call(s32[64]{0:T(128)} %start_hbm.1, s32[64]{0:T(128)} %end_hbm.1, f32[16,32768]{1,0:T(8,128)} %sig_hbm.1), custom_call_target="tpu_custom_call" | custom-call | tf_op jit(solution)/shard_map/pallas_call | solution.py:538
  33.6 2.0 %shard_map.59 = (f32[16,32768]{1,0:T(8,128)}, f32[16,32768]{1,0:T(8,128)}, f32[16,64]{1,0:T(8,128)}) custom-call(f32[16,32768]{1,0:T(8,128)S(1)} %get-tuple-element.7.smooth, f32[16,32768]{1,0:T(8,128)S(1)} %get-tuple-element.8.slope, f32[32,8,128]{2,1,0:T(8,128)S(1)} %get-tuple-element.9.shares, f32[8,128]{1,0:T(8,128)S(1)} %get-tuple-element.10.count), custom_call_target="tpu_custom_call" | custom-call | tf_op jit(solution)/shard_map/pallas_call | solution.py:575

commit v6 on v5

--- a/solution.py
+++ b/solution.py
@@ -315,32 +315,32 @@
             greeting(1)
 
         if not swaps:
-            @pl.when((k >= 1) & (k <= sends))
+            @pl.when(k < sends)
             def _():
-                transfer(k - 1).start()
+                transfer(k).start()
 
             return carry
 
-        @pl.when((k == detour) & side_from)
+        @pl.when((k == detour - 1) & side_from)
         def _():
             aside().start()
 
-        @pl.when((k == detour + 1) & whole_from)
-        def _():
-            away(k - 1, 0).start()
-
-        @pl.when((k == detour + 2) & half_from)
-        def _():
-            away(k - 1, 1).start()
+        @pl.when((k == detour) & whole_from)
+        def _():
+            away(k, 0).start()
+
+        @pl.when((k == detour + 1) & half_from)
+        def _():
+            away(k, 1).start()
 
         @pl.when((k == per + lag) & side_to)
         def _():
             aside().wait_recv()
             over().start()
 
-        m = jnp.where(k <= per, k - 1, k - 1 - lag)
+        m = jnp.where(k < per, k, k - lag)
         fork, split = (m == detour - 1) & side_from, (m == detour + 1) & half_from
-        ready = ((k >= 1) & (k <= per)) | ((k > per + lag) & (m < sends))
+        ready = (k < per) | ((k >= per + lag) & (m < sends))
 
         @pl.when(ready & jnp.logical_not(fork | split | ((m == detour) & whole_from)))
         def _():
@@ -365,7 +365,7 @@
         return move
 
     if swaps:
-        for m in range(steps - 1 - lag, sends):
+        for m in range(steps - lag, sends):
             transfer(m).start()
         pl.when(whole_to)(pass_on(0))
         pl.when(half_to)(pass_on(1))
@@ -410,10 +410,10 @@
 
     for g in range(n_s):
         part[g] = pack(both[g * rows : (g + 1) * rows])
-        if g < 2:
-            @pl.when((t != 0) | (s != g))
-            def _():
-                early(g).start()
+    for g in range(2):
+        @pl.when((t != 0) | (s != g))
+        def _():
+            early(g).start()
 
 
     core = lax.rem(s, 2)

time: 35.8 us -> 35.2 us (0.983)
  Pallas kernels: 35 us -> 34.4 us
    pallas_call x1, Pallas kernels: 32.9 us -> 32.4 us  [shards(): pl.pallas_call(functools.partial(kernel, n_s, n_t, rows, width, chunk), o...]
where the time goes in v6:
time: 35.2 us; the launch traced here: 35.1 us
  Pallas kernels  34.4 us (98%)
  between operations  0.64 us (2%)
    pallas_call x1, Pallas kernels, shards(): pl.pallas_call(functools.partial(kernel, n_s, n_t, rows, width, chunk), o...  32.4 us
    pallas_call x1, Pallas kernels, shards(): pl.pallas_call(flush, out_shape=tuple((jax.ShapeDtypeStruct(v, f32) for v...  2.04 us

profile of v6, /device:TPU:0, one launch (start us, length us, event | category | flops | bytes accessed | tf_op | source)
XLA Modules:
  0.0 35.1 jit_solution(9176021620734704642)
XLA Ops:
  0.6 32.4 %shard_map.58 = (f32[16,32768]{1,0:T(8,128)S(1)}, f32[16,32768]{1,0:T(8,128)S(1)}, f32[32,8,128]{2,1,0:T(8,128)S(1)}, f32[8,128]{1,0:T(8,128)S(1)}) custom-call(s32[64]{0:T(128)} %start_hbm.1, s32[64]{0:T(128)} %end_hbm.1, f32[16,32768]{1,0:T(8,128)} %sig_hbm.1), custom_call_target="tpu_custom_call" | custom-call | tf_op jit(solution)/shard_map/pallas_call | solution.py:538
  33.0 2.0 %shard_map.59 = (f32[16,32768]{1,0:T(8,128)}, f32[16,32768]{1,0:T(8,128)}, f32[16,64]{1,0:T(8,128)}) custom-call(f32[16,32768]{1,0:T(8,128)S(1)} %get-tuple-element.7.smooth, f32[16,32768]{1,0:T(8,128)S(1)} %get-tuple-element.8.slope, f32[32,8,128]{2,1,0:T(8,128)S(1)} %get-tuple-element.9.shares, f32[8,128]{1,0:T(8,128)S(1)} %get-tuple-element.10.count), custom_call_target="tpu_custom_call" | custom-call | tf_op jit(solution)/shard_map/pallas_call | solution.py:575

commit v7 on v6

--- a/solution.py
+++ b/solution.py
@@ -184,9 +184,30 @@
     def column(j):
         return pl.multiple_of(j * chunk, chunk)
 
+    tail = chunk // 4
+
+    def closing(k, at, size, sem):
+        q, j = place(k)
+        return pltpu.make_async_remote_copy(
+            res.at[:, pl.ds(column(q * per + j) + at, size)], mixed.at[s, :, pl.ds(column(j) + at, size)],
+            send_sem, recv_sem.at[sem],
+            device_id={"series": q}, device_id_type=MESH)
+
+    def send(k):
+        ends_here = lax.rem(k, per) == per - 1
+
+        @pl.when(jnp.logical_not(ends_here))
+        def _():
+            transfer(k).start()
+
+        @pl.when(ends_here)
+        def _():
+            closing(k, 0, chunk - tail, 0).start()
+            closing(k, chunk - tail, tail, per).start()
+
     def away(k, n):
         q, j = place(k)
-        size = chunk if n == 0 else chunk // 2
+        size = chunk if n == 0 else chunk // 4
         return pltpu.make_async_remote_copy(
             res.at[:, pl.ds(column(q * per + j), size)], relay.at[0, :, pl.ds(0, size)],
             send_sem, relay_recv.at[0],
@@ -194,7 +215,7 @@
 
     def onward(n):
         j = detour + n - per + 1
-        size = chunk if n == 0 else chunk // 2
+        size = chunk if n == 0 else chunk // 4
         return pltpu.make_async_remote_copy(
             relay.at[0, :, pl.ds(0, size)], mixed.at[across, :, pl.ds(j * chunk, size)],
             relay_send.at[0], recv_sem.at[j],
@@ -317,7 +338,7 @@
         if not swaps:
             @pl.when(k < sends)
             def _():
-                transfer(k).start()
+                send(k)
 
             return carry
 
@@ -344,7 +365,7 @@
 
         @pl.when(ready & jnp.logical_not(fork | split | ((m == detour) & whole_from)))
         def _():
-            transfer(m).start()
+            send(m)
 
         @pl.when(ready & fork)
         def _():
@@ -352,7 +373,7 @@
 
         @pl.when(ready & split)
         def _():
-            rest(m, chunk // 2).start()
+            rest(m, chunk // 4).start()
 
         return carry
 
@@ -366,15 +387,14 @@
 
     if swaps:
         for m in range(steps - lag, sends):
-            transfer(m).start()
+            send(m)
         pl.when(whole_to)(pass_on(0))
         pl.when(half_to)(pass_on(1))
 
-    def arrival(i):
-        j = (i + 1) % per
-        block = mixed.at[pl.ds(0, n_s - 1), :, pl.ds(pl.multiple_of(j * chunk, chunk), chunk)]
-        return pltpu.make_async_remote_copy(
-            block, block, send_sem, recv_sem.at[j],
+    def arrival(at, size, sem):
+        block = mixed.at[pl.ds(0, n_s - 1), :, pl.ds(at, size)]
+        return pltpu.make_async_remote_copy(
+            block, block, send_sem, recv_sem.at[sem],
             device_id={"series": lax.rem(s + 1, n_s)}, device_id_type=MESH)
 
     half = rows // 2
@@ -384,17 +404,17 @@
         return jnp.where(left_half, v[:half], v[half:])
 
     gram = jnp.zeros((2 * total, 2 * total), f32)
-    for i in range(per):
+    parts = [(j * chunk, chunk, j) for j in range(1, per)]
+    parts += [(0, chunk - tail, 0), (chunk - tail, tail, per)]
+    for i, (at, size, sem) in enumerate(parts):
         greeting(i + 2)
-        arrival(i).wait_recv()
-        j = (i + 1) % per
-        x = jnp.concatenate(
-            [mixed[g, :, pl.ds(pl.multiple_of(j * chunk, chunk), chunk)] for g in range(n_s)], axis=0)
+        arrival(at, size, sem).wait_recv()
+        x = jnp.concatenate([mixed[g, :, at : at + size] for g in range(n_s)], axis=0)
         hi = x.astype(jnp.bfloat16)
         lo = (x - hi.astype(f32)).astype(jnp.bfloat16)
         z = jnp.concatenate([hi, lo], axis=0)
         gram = gram + lax.dot_general(z, z, (((1,), (1,)), ((), ())), preferred_element_type=f32)
-    for i in range(per + 2, len(rounds) + 1):
+    for i in range(per + 3, len(rounds) + 1):
         greeting(i)
     both = gram[:total] + gram[total:]
     both = both + pltpu.roll(both, total, 1)
@@ -562,7 +582,7 @@
                 dma((2,)),
                 dma((2,)),
                 dma,
-                dma((per,)),
+                dma((per + 1,)),
                 dma((2,)),
                 pltpu.SemaphoreType.REGULAR((1 + len(rounds_of(n_t)),)),
                 dma((2,)),

time: 35.2 us -> 35 us (level)
  no operation moved by 1% of the time
where the time goes in v7:
time: 35 us; the launch traced here: 34.8 us
  Pallas kernels  34.2 us (98%)
  between operations  0.64 us (2%)
    pallas_call x1, Pallas kernels, shards(): pl.pallas_call(functools.partial(kernel, n_s, n_t, rows, width, chunk), o...  32.1 us
    pallas_call x1, Pallas kernels, shards(): pl.pallas_call(flush, out_shape=tuple((jax.ShapeDtypeStruct(v, f32) for v...  2.04 us

profile of v7, /device:TPU:0, one launch (start us, length us, event | category | flops | bytes accessed | tf_op | source)
XLA Modules:
  0.0 34.8 jit_solution(12769669468037188968)
XLA Ops:
  0.6 32.1 %shard_map.58 = (f32[16,32768]{1,0:T(8,128)S(1)}, f32[16,32768]{1,0:T(8,128)S(1)}, f32[32,8,128]{2,1,0:T(8,128)S(1)}, f32[8,128]{1,0:T(8,128)S(1)}) custom-call(s32[64]{0:T(128)} %start_hbm.1, s32[64]{0:T(128)} %end_hbm.1, f32[16,32768]{1,0:T(8,128)} %sig_hbm.1), custom_call_target="tpu_custom_call" | custom-call | tf_op jit(solution)/shard_map/pallas_call | solution.py:558
  32.8 2.0 %shard_map.59 = (f32[16,32768]{1,0:T(8,128)}, f32[16,32768]{1,0:T(8,128)}, f32[16,64]{1,0:T(8,128)}) custom-call(f32[16,32768]{1,0:T(8,128)S(1)} %get-tuple-element.7.smooth, f32[16,32768]{1,0:T(8,128)S(1)} %get-tuple-element.8.slope, f32[32,8,128]{2,1,0:T(8,128)S(1)} %get-tuple-element.9.shares, f32[8,128]{1,0:T(8,128)S(1)} %get-tuple-element.10.count), custom_call_target="tpu_custom_call" | custom-call | tf_op jit(solution)/shard_map/pallas_call | solution.py:595

commit v8 on v7

--- a/solution.py
+++ b/solution.py
@@ -178,7 +178,7 @@
         return pltpu.make_async_remote_copy(
             res.at[:, pl.ds(pl.multiple_of(q * quarter + j * chunk, chunk), chunk)],
             mixed.at[s, :, pl.ds(pl.multiple_of(j * chunk, chunk), chunk)],
-            send_sem, recv_sem.at[j],
+            send_sem, recv_sem.at[(j + 1) // 2 if isinstance(j, int) else lax.div(j + 1, 2)],
             device_id={"series": q}, device_id_type=MESH)
 
     def column(j):
@@ -203,7 +203,7 @@
         @pl.when(ends_here)
         def _():
             closing(k, 0, chunk - tail, 0).start()
-            closing(k, chunk - tail, tail, per).start()
+            closing(k, chunk - tail, tail, per // 2 + 1).start()
 
     def away(k, n):
         q, j = place(k)
@@ -218,7 +218,7 @@
         size = chunk if n == 0 else chunk // 4
         return pltpu.make_async_remote_copy(
             relay.at[0, :, pl.ds(0, size)], mixed.at[across, :, pl.ds(j * chunk, size)],
-            relay_send.at[0], recv_sem.at[j],
+            relay_send.at[0], recv_sem.at[(j + 1) // 2 if isinstance(j, int) else lax.div(j + 1, 2)],
             device_id={"tm": mirror}, device_id_type=MESH)
 
     def aside():
@@ -232,7 +232,7 @@
         j = detour - per
         return pltpu.make_async_remote_copy(
             relay.at[1, :, pl.ds(0, slip)], mixed.at[s, :, pl.ds(j * chunk, slip)],
-            relay_send.at[1], recv_sem.at[j],
+            relay_send.at[1], recv_sem.at[(j + 1) // 2 if isinstance(j, int) else lax.div(j + 1, 2)],
             device_id={"series": across, "tm": partner}, device_id_type=MESH)
 
     def rest(k, at):
@@ -240,7 +240,7 @@
         return pltpu.make_async_remote_copy(
             res.at[:, pl.ds(column(q * per + j) + at, chunk - at)],
             mixed.at[s, :, pl.ds(column(j) + at, chunk - at)],
-            send_sem, recv_sem.at[j],
+            send_sem, recv_sem.at[(j + 1) // 2 if isinstance(j, int) else lax.div(j + 1, 2)],
             device_id={"series": q}, device_id_type=MESH)
 
     def greeting(i):
@@ -404,8 +404,8 @@
         return jnp.where(left_half, v[:half], v[half:])
 
     gram = jnp.zeros((2 * total, 2 * total), f32)
-    parts = [(j * chunk, chunk, j) for j in range(1, per)]
-    parts += [(0, chunk - tail, 0), (chunk - tail, tail, per)]
+    parts = [(j * chunk, min(2, per - j) * chunk, (j + 1) // 2) for j in range(1, per, 2)]
+    parts += [(0, chunk - tail, 0), (chunk - tail, tail, per // 2 + 1)]
     for i, (at, size, sem) in enumerate(parts):
         greeting(i + 2)
         arrival(at, size, sem).wait_recv()
@@ -414,7 +414,7 @@
         lo = (x - hi.astype(f32)).astype(jnp.bfloat16)
         z = jnp.concatenate([hi, lo], axis=0)
         gram = gram + lax.dot_general(z, z, (((1,), (1,)), ((), ())), preferred_element_type=f32)
-    for i in range(per + 3, len(rounds) + 1):
+    for i in range(len(parts) + 2, len(rounds) + 1):
         greeting(i)
     both = gram[:total] + gram[total:]
     both = both + pltpu.roll(both, total, 1)
@@ -582,7 +582,7 @@
                 dma((2,)),
                 dma((2,)),
                 dma,
-                dma((per + 1,)),
+                dma((per // 2 + 2,)),
                 dma((2,)),
                 pltpu.SemaphoreType.REGULAR((1 + len(rounds_of(n_t)),)),
                 dma((2,)),

time: 35 us -> 34.9 us (level)
  no operation moved by 1% of the time
where the time goes in v8:
time: 34.9 us; the launch traced here: 34.8 us
  Pallas kernels  34.2 us (98%)
  between operations  0.64 us (2%)
    pallas_call x1, Pallas kernels, shards(): pl.pallas_call(functools.partial(kernel, n_s, n_t, rows, width, chunk), o...  32.1 us
    pallas_call x1, Pallas kernels, shards(): pl.pallas_call(flush, out_shape=tuple((jax.ShapeDtypeStruct(v, f32) for v...  2.04 us

profile of v8, /device:TPU:0, one launch (start us, length us, event | category | flops | bytes accessed | tf_op | source)
XLA Modules:
  0.0 34.8 jit_solution(15509648865426604263)
XLA Ops:
  0.6 32.1 %shard_map.58 = (f32[16,32768]{1,0:T(8,128)S(1)}, f32[16,32768]{1,0:T(8,128)S(1)}, f32[32,8,128]{2,1,0:T(8,128)S(1)}, f32[8,128]{1,0:T(8,128)S(1)}) custom-call(s32[64]{0:T(128)} %start_hbm.1, s32[64]{0:T(128)} %end_hbm.1, f32[16,32768]{1,0:T(8,128)} %sig_hbm.1), custom_call_target="tpu_custom_call" | custom-call | tf_op jit(solution)/shard_map/pallas_call | solution.py:558
  32.8 2.0 %shard_map.59 = (f32[16,32768]{1,0:T(8,128)}, f32[16,32768]{1,0:T(8,128)}, f32[16,64]{1,0:T(8,128)}) custom-call(f32[16,32768]{1,0:T(8,128)S(1)} %get-tuple-element.7.smooth, f32[16,32768]{1,0:T(8,128)S(1)} %get-tuple-element.8.slope, f32[32,8,128]{2,1,0:T(8,128)S(1)} %get-tuple-element.9.shares, f32[8,128]{1,0:T(8,128)S(1)} %get-tuple-element.10.count), custom_call_target="tpu_custom_call" | custom-call | tf_op jit(solution)/shard_map/pallas_call | solution.py:595
